TPU v7x, 32 devices: a 4x4x1 block of a 4x4x8 slice. The times are simulated.
32 devices in a mesh: rep: 1 (over z), dp: 32 (over x, y, core).
Axes of the slice: x: 4, y: 4, z: 1, core: 2. Of those that a mesh axis runs over, the one named last changes fastest.
The devices are a block of a 4x4x8 slice.
Arguments:
- g_w_gate: bfloat16 [32, 2, 1280, 4480], P(('rep', 'dp'))
- g_w_up: bfloat16 [32, 2, 1280, 4480], P(('rep', 'dp'))
- g_w_down: bfloat16 [32, 2, 4480, 1280], P(('rep', 'dp'))
- w_gate: bfloat16 [2, 1280, 4480], replicated
- w_up: bfloat16 [2, 1280, 4480], replicated
- w_down: bfloat16 [2, 4480, 1280], replicated
- m_w_gate: float32 [2, 1280, 4480], P(None, 'dp')
- m_w_up: float32 [2, 1280, 4480], P(None, 'dp')
- m_w_down: float32 [2, 4480, 1280], P(None, 'dp')
- v_w_gate: float32 [2, 1280, 4480], P(None, 'dp')
- v_w_up: float32 [2, 1280, 4480], P(None, 'dp')
- v_w_down: float32 [2, 4480, 1280], P(None, 'dp')
Outputs:
- output 1: bfloat16 [2, 1280, 4480], P('rep')
- output 2: bfloat16 [2, 1280, 4480], P('rep')
- output 3: bfloat16 [2, 4480, 1280], P('rep')
- output 4: float32 [2, 1280, 4480], P('rep', 'dp')
- output 5: float32 [2, 1280, 4480], P('rep', 'dp')
- output 6: float32 [2, 4480, 1280], P('rep', 'dp')
- output 7: float32 [2, 1280, 4480], P('rep', 'dp')
- output 8: float32 [2, 1280, 4480], P('rep', 'dp')
- output 9: float32 [2, 4480, 1280], P('rep', 'dp')
All inputs are finite; a program needn't handle non-finite values.
Results may differ from a plain program's by a relative error of at most 0.022.
Values are sent between devices in bfloat16 or wider.
A program may use at most 768 MiB of HBM per device.

v0:
```python
import jax
import jax.numpy as jnp
from jax import lax
from jax.sharding import PartitionSpec as P


def adamw(w, m, v, g):
    m = 0.9 * m + 0.1 * g
    v = 0.95 * v + 0.05 * g * g
    step = m * lax.rsqrt(v + 1e-8) + 0.1 * w
    return (w - 0.02 * step).astype(jnp.bfloat16), m, v


def solution(mesh):
    def step(*arrays):
        terms, weights, m, v = (arrays[i : i + 3] for i in (0, 3, 6, 9))
        gradients = [lax.psum_scatter(t[0], "dp", scatter_dimension=1, tiled=True).astype(jnp.float32) for t in terms]
        me = lax.axis_index("dp")
        own = [lax.dynamic_slice_in_dim(w, me * one.shape[1], one.shape[1], 1).astype(jnp.float32) for w, one in zip(weights, m, strict=True)]
        new = [adamw(w, m, v, g) for w, m, v, g in zip(own, m, v, gradients, strict=True)]
        whole = [lax.all_gather(one[0], "dp", axis=1, tiled=True) for one in new]
        return (*whole, *(one[1] for one in new), *(one[2] for one in new))

    all_of, cut = P(None, None, None), P(None, "dp", None)
    return jax.shard_map(
        step,
        mesh=mesh,
        in_specs=(P(("rep", "dp"), None, None, None),) * 3 + (all_of,) * 3 + (cut,) * 6,
        out_specs=(P("rep", None, None),) * 3 + (P("rep", "dp", None),) * 6,
        check_vma=False,
    )
```

profile of v0, /device:TPU:97, one launch (start us, length us, event | category | flops | bytes accessed | tf_op | source)
XLA Modules:
  0.0 847.9 jit_solution(4535152452019173718)
XLA Ops:
  7.2 0.1 all-reduce.3.cloned.1.call-start
  7.3 105.1 %copy.44 = bf16[1,2,4480,1280]{3,1,2,0:T(2,128)(2,1)} copy(bf16[1,2,4480,1280]{3,2,1,0:T(8,128)(2,1)} %param.14) | data formatting | bytes 45875200 | tf_op args[2]
  112.4 0.1 all-reduce.3.cloned.1.call-update
  112.4 0.1 reduce-scatter.7.cloned.1.call-start
  112.5 99.5 %copy.27 = bf16[2,1280,4480]{2,0,1:T(2,128)(2,1)S(1)} copy(bf16[2,1280,4480]{2,1,0:T(8,128)(2,1)} %bitcast.18) | data formatting | bytes 45875200
  212.0 8.0 copy.32
  219.9 0.1 reduce-scatter.7.cloned.1.call-update
  220.0 0.1 reduce-scatter.9.cloned.1.call-start
  220.1 99.5 %copy.29 = bf16[2,1280,4480]{2,0,1:T(2,128)(2,1)S(1)} copy(bf16[2,1280,4480]{2,1,0:T(8,128)(2,1)} %bitcast.19) | data formatting | bytes 45875200
  319.5 8.0 copy.33
  327.5 0.1 reduce-scatter.9.cloned.1.call-update
  327.6 0.1 all-gather.8.cloned.1.call-start
  327.6 1.4 constant_dynamic-slice_fusion
  329.1 0.1 copy-done.3
  329.2 7.0 fusion.14
  336.2 0.1 all-gather.8.cloned.1.call-update
  336.2 0.2 all-gather.4.cloned.1.call-start
  336.5 92.5 %reduce-scatter.7.cloned.1.call-done = bf16[40,8960]{1,0:T(8,128)(2,1)} async-done(((bf16[1280,8960]{1,0:T(8,128)(2,1)}), bf16[40,8960]{1,0:T(8,128)(2,1)}) %reduce-scatter.7.cloned.1.call-update) | async-done | bytes 716816
  429.0 2.1 reshape.19
  431.1 3.7 fusion.2
  434.8 0.1 all-gather.4.cloned.1.call-update
  434.9 0.1 all-gather.6.cloned.1.call-start
  434.9 124.8 %reduce-scatter.9.cloned.1.call-done = bf16[40,8960]{1,0:T(8,128)(2,1)} async-done(((bf16[1280,8960]{1,0:T(8,128)(2,1)}), bf16[40,8960]{1,0:T(8,128)(2,1)}) %reduce-scatter.9.cloned.1.call-update) | async-done | bytes 716816
  559.7 2.1 reshape.21
  561.8 3.7 fusion.6
  565.6 77.9 %all-gather.8.cloned.1.call-done = bf16[2,4480,1280]{2,0,1:T(2,128)(2,1)} async-done(((bf16[2,140,1280]{2,0,1:T(2,128)(2,1)}), bf16[2,4480,1280]{2,0,1:T(2,128)(2,1)}) %all-gather.8.cloned.1.call-update) | async-done | bytes 22937616 | tf_op jit(solution)/shard_map/all_gather | solution.py:21
  643.5 22.7 %copy.26 = bf16[2,4480,1280]{2,1,0:T(8,128)(2,1)} copy(bf16[2,4480,1280]{2,0,1:T(2,128)(2,1)} %all-gather.8.cloned.1.call-done) | data formatting | bytes 45875200
  666.2 60.7 %all-gather.4.cloned.1.call-done = bf16[2,1280,4480]{2,1,0:T(8,128)(2,1)} async-done(((bf16[2,40,4480]{2,1,0:T(8,128)(2,1)}), bf16[2,1280,4480]{2,1,0:T(8,128)(2,1)}) %all-gather.4.cloned.1.call-update) | async-done | bytes 22937616 | tf_op jit(solution)/shard_map/all_gather | solution.py:21
  726.9 83.4 %all-gather.6.cloned.1.call-done = bf16[2,1280,4480]{2,1,0:T(8,128)(2,1)} async-done(((bf16[2,40,4480]{2,1,0:T(8,128)(2,1)}), bf16[2,1280,4480]{2,1,0:T(8,128)(2,1)}) %all-gather.6.cloned.1.call-update) | async-done | bytes 22937616 | tf_op jit(solution)/shard_map/all_gather | solution.py:21
  810.3 15.8 %copy.48 = bf16[2,1280,4480]{2,1,0:T(8,128)(2,1)} copy(bf16[2,1280,4480]{2,1,0:T(8,128)(2,1)} %all-gather.4.cloned.1.call-done) | data formatting | bytes 45875200
  826.1 6.7 copy-done
  832.8 8.2 copy.49
  (8 shorter events, 0.1 us)
Async XLA Ops:
  7.2 321.9 %all-reduce.3.cloned.1.call-start = ((), (), s32[]{:S(2)}) async-start(), calls=%async_computation.7 | async-start | bytes 45875200
  112.4 316.5 %reduce-scatter.7.cloned.1.call-start = ((), (), s32[]{:S(2)}) async-start(), calls=%async_computation.5 | async-start | bytes 23654400
  220.0 339.7 %reduce-scatter.9.cloned.1.call-start = ((), (), s32[]{:S(2)}) async-start(), calls=%async_computation.6 | async-start | bytes 23654400
  327.6 1.6 copy-start.3
  327.6 316.0 %all-gather.8.cloned.1.call-start = ((), (), s32[]{:S(2)}) async-start(), calls=%async_computation.4 | async-start | bytes 23654400 | tf_op jit(solution)/shard_map/all_gather | solution.py:21
  336.2 94.9 %copy-start.1 = (f32[2,40,4480]{2,1,0:T(8,128)S(1)}, f32[2,40,4480]{2,1,0:T(8,128)}, u32[]{:S(2)}) copy-start(f32[2,40,4480]{2,1,0:T(8,128)} %param.21) | copy-start | bytes 4300804
  336.2 390.7 %all-gather.4.cloned.1.call-start = ((), (), s32[]{:S(2)}) async-start(), calls=%async_computation.2 | async-start | bytes 23654400 | tf_op jit(solution)/shard_map/all_gather | solution.py:21
  434.8 127.0 %copy-start.2 = (f32[2,40,4480]{2,1,0:T(8,128)S(1)}, f32[2,40,4480]{2,1,0:T(8,128)}, u32[]{:S(2)}) copy-start(f32[2,40,4480]{2,1,0:T(8,128)} %param.22) | copy-start | bytes 4300804
  434.9 375.4 %all-gather.6.cloned.1.call-start = ((), (), s32[]{:S(2)}) async-start(), calls=%async_computation.3 | async-start | bytes 23654400 | tf_op jit(solution)/shard_map/all_gather | solution.py:21
  810.3 22.5 %copy-start = (bf16[2,1280,4480]{2,1,0:T(8,128)(2,1)S(1)}, bf16[2,1280,4480]{2,1,0:T(8,128)(2,1)}, u32[]{:S(2)}) copy-start(bf16[2,1280,4480]{2,1,0:T(8,128)(2,1)} %all-gather.6.cloned.1.call-done) | copy-start | bytes 68812800
Sparse Core Ops, SparseCore 0:
  112.6 186.2 all-reduce.2
  303.3 125.6 reduce-scatter.6
  433.4 126.2 reduce-scatter.8
  561.7 81.7 all-gather.7
  646.1 80.7 all-gather.3
  729.5 80.7 all-gather.5
where the time goes:
time: 848 us
  waiting for transfers between devices  440 us (52%)
  local copies, waits for them, and re-layouts  379 us (45%)
  other arithmetic  14.5 us (2%)
  between operations  14.2 us (2%)
    unnamed x18, local copies, waits for them, and re-layouts  378 us
    all_gather x3, waiting for transfers between devices, step(): whole = [lax.all_gather(one[0], 'dp', axis=1, tiled=True) for one in new]  222 us
    unnamed x9, waiting for transfers between devices  218 us
  transfers between devices with their start and end apart: 6, of which 5 were waited for; matrix products, arithmetic and copies ran while one was open for 30% of the time, Pallas kernels for 0%

commit v1 on v0

v1 whole, which is shorter than its diff:
```python
import functools
import math

import jax
import jax.numpy as jnp
from jax import lax
from jax.experimental import pallas as pl
from jax.experimental.pallas import tpu as pltpu
from jax.sharding import PartitionSpec as P

MESH = pl.DeviceIdType.MESH
F32, BF16 = jnp.float32, jnp.bfloat16
CORES, SIDE = 2, 4
WEIGHTS = 3
ROWS, COLS = 40, 640
LAG = (0, 1, 2, 3, 4)
SLOTS = LAG[4] + LAG[2] + 2
HELD = LAG[4] + 2
SENT = 3
AHEAD = 3


def fused(pieces, *refs):
    (gd, gg, gu, wd, wg, wu, md, vd, mg, vg, mu, vu, whole, sum_d, sum_g, sum_u, theirs,
     own, par, r1, r2, u1, u2, s1, s2, t1, t2, total, new, got3, gotm, put3, putm, newm, mbd, vbd, wb3, wbm, mbg, vbg, wbg,
     sem_load, sem_swap_s, sem_swap_r, sem_r1, sem_r2, sem_u1, sem_u2, sem_s1, sem_s2, sem_t1, sem_t2,
     sem_m, sem_out, sem_xs, sem_xr, sem_own, sem_gs, sem_gr, sem_os, sem_or) = refs
    count = WEIGHTS * pieces
    me = lax.axis_index("dp")
    x, y, c = me // (CORES * SIDE), (me // CORES) % SIDE, me % CORES
    other = 1 - c

    def dev(x, y, c):
        return ((x % SIDE) * SIDE + y % SIDE) * CORES + c

    partner = dev(x, y, other)
    place = ((x, y), (y, x))

    def dev_i(t, d):
        return dev(x + d, y, c) if t == 0 else dev(x, y + d, c)

    def dev_j(t, d):
        return dev_i(1 - t, d)

    def at(t, i, j):
        return (i % SIDE, j % SIDE) if t == 0 else (j % SIDE, i % SIDE)

    def send(src, dst, ssem, rsem, to):
        return pltpu.make_async_remote_copy(src_ref=src, dst_ref=dst, send_sem=ssem, recv_sem=rsem, device_id={"dp": to}, device_id_type=MESH)

    def wait(ref, sem):
        pltpu.make_async_copy(ref, ref, sem).wait()

    def of_weight(q, do):
        for w in range(WEIGHTS):
            @pl.when(q // pieces == w)
            def _(w=w):
                do(w, q % pieces)

    def term(w, t, p, core):
        if w == 0:
            return gd.at[t, :, :, pl.ds(pl.multiple_of(p * ROWS, 8), ROWS), pl.ds(pl.multiple_of(core * COLS, 128), COLS)]
        return (gg, gu)[w - 1].at[t, :, :, core, :, pl.ds(pl.multiple_of(p * COLS, 128), COLS)]

    def swap(q):
        def do(w, p):
            for t in range(2):
                send(term(w, t, p, other), theirs.at[q, t], sem_swap_s.at[t], sem_swap_r.at[q, t], partner).start()
        of_weight(q, do)

    def load(q):
        def do(w, p):
            for t in range(2):
                pltpu.make_async_copy(term(w, t, p, c), own.at[q % HELD, t], sem_load.at[0, t, q % 2]).start()
        of_weight(q, do)
        for t in range(2):
            wait(theirs.at[q, t], sem_swap_r.at[q, t])
            pltpu.make_async_copy(theirs.at[q, t], par.at[q % HELD, t], sem_load.at[1, t, q % 2]).start()

    def add(dst, *srcs):
        for k in range(COLS // 128):
            cut = (slice(None), slice(128 * k, 128 * k + 128))
            value = srcs[0][cut].astype(F32)
            for src in srcs[1:]:
                value = value + src[cut].astype(F32)
            dst[cut] = value.astype(dst.dtype)

    def both(q, t, i, j):
        a, b = at(t, i, j)
        return own.at[q % HELD, t, a, b], par.at[q % HELD, t, a, b]

    def freed(buf, sem, q):
        @pl.when(q >= SENT)
        def _():
            wait(buf, sem)

    def first(q, t, d):
        z, r = q % SENT, q % SLOTS
        return send(s1.at[z, t, d], r1.at[r, t, d], sem_s1.at[z, t, d], sem_r1.at[r, t, d], dev_i(t, (1, 3)[d]))

    def second(q, t, d, h):
        z, r = q % SENT, q % SLOTS
        return send(s2.at[z, t, d, h], r2.at[r, t, d, h], sem_s2.at[z, t, d, h], sem_r2.at[r, t, d, h], dev_i(t, (1, 3)[d]))

    def stage0(q):
        z = q % SENT
        for t in range(2):
            wait(own.at[q % HELD, t], sem_load.at[0, t, q % 2])
            wait(par.at[q % HELD, t], sem_load.at[1, t, q % 2])
        for t in range(2):
            i = place[t][0]
            for d in range(2):
                freed(s1.at[z, t, d], sem_s1.at[z, t, d], q)
                for b in range(2):
                    add(s1.at[z, t, d, b], *both(q, t, i + 2, 2 * d + b))
            for d in range(2):
                first(q, t, d).start()
        for t in range(2):
            i = place[t][0]
            for d in range(2):
                freed(s2.at[z, t, d, 1 - d], sem_s2.at[z, t, d, 1 - d], q)
                for b in range(2):
                    add(s2.at[z, t, d, 1 - d, b], *both(q, t, i + (1, 3)[d], 2 * (1 - d) + b))
            for d in range(2):
                second(q, t, d, 1 - d).start()

    def stage1(q):
        z, r = q % SENT, q % SLOTS
        for t in range(2):
            i = place[t][0]
            for d in range(2):
                freed(s2.at[z, t, d, d], sem_s2.at[z, t, d, d], q)
                wait(r1.at[r, t, d], sem_r1.at[r, t, d])
                for b in range(2):
                    add(s2.at[z, t, d, d, b], r1.at[r, t, d, b], *both(q, t, i + (1, 3)[d], 2 * d + b))
            for d in range(2):
                second(q, t, d, d).start()

    def cell(q, t, j):
        r, j = q % SLOTS, j % SIDE
        return (r2.at[r, t, 0, j // 2, j % 2], r2.at[r, t, 1, j // 2, j % 2], *both(q, t, place[t][0], j))

    def side(q):
        return 1 + 2 * (q % 2)

    def far(q, t):
        z, r = q % SENT, q % SLOTS
        return send(t1.at[z, t], u1.at[r, t], sem_t1.at[z, t], sem_u1.at[r, t], dev_j(t, side(q)))

    def near(q, t, e):
        z, r = q % SENT, q % SLOTS
        to = (side(q), SIDE - side(q))[e]
        return send(t2.at[z, t, e], u2.at[r, t, e], sem_t2.at[z, t, e], sem_u2.at[r, t, e], dev_j(t, to))

    def stage2(q):
        z, r = q % SENT, q % SLOTS
        for t in range(2):
            j = place[t][1]
            for d in range(2):
                for h in range(2):
                    wait(r2.at[r, t, d, h], sem_r2.at[r, t, d, h])
            freed(t1.at[z, t], sem_t1.at[z, t], q)
            freed(t2.at[z, t, 1], sem_t2.at[z, t, 1], q)
            add(t1.at[z, t], *cell(q, t, j + 2))
            add(t2.at[z, t, 1], *cell(q, t, j + SIDE - side(q)))
            far(q, t).start()
            near(q, t, 1).start()

    def stage3(q):
        z, r = q % SENT, q % SLOTS
        for t in range(2):
            freed(t2.at[z, t, 0], sem_t2.at[z, t, 0], q)
            wait(u1.at[r, t], sem_u1.at[r, t])
            add(t2.at[z, t, 0], u1.at[r, t], *cell(q, t, place[t][1] + side(q)))
            near(q, t, 0).start()

    def stage4(q):
        r = q % SLOTS
        for t in range(2):
            for e in range(2):
                wait(u2.at[r, t, e], sem_u2.at[r, t, e])
            add(total.at[q, t], u2.at[r, t, 0], u2.at[r, t, 1], *cell(q, t, place[t][1]))

    def adamw(dst, w, m, v, g):
        w, g = w.astype(F32), g.astype(F32)
        m = 0.9 * m + 0.1 * g
        v = 0.95 * v + 0.05 * g * g
        step = m * lax.rsqrt(v + 1e-8) + 0.1 * w
        dst[...] = (w - 0.02 * step).astype(BF16)

    third, mid = pieces // 2, 24
    top, cut = pieces * ROWS // 2 - third * ROWS, 16

    def parts(core):
        return [((third + 1) * core + k, 0, pl.multiple_of(mid * core + ROWS * k, 8), ROWS) for k in range(third)] + [
            (third, pl.multiple_of(cut * core, 16), pl.multiple_of(third * ROWS * (1 - core), 8), mid)]

    def loads_d():
        copies = [pltpu.make_async_copy(md, mbd, sem_m.at[0]), pltpu.make_async_copy(vd, vbd, sem_m.at[1])]
        rows = pl.ds(pl.multiple_of((third + 1) * ROWS * c, 8), third * ROWS)
        for t in range(2):
            copies.append(pltpu.make_async_copy(wd.at[t, x, y, rows], wb3.at[t], sem_m.at[2 + t]))
            rest = pl.ds(pl.multiple_of(third * ROWS + cut * c, 8), mid)
            copies.append(pltpu.make_async_copy(wd.at[t, x, y, rest], wbm.at[t], sem_m.at[4 + t]))
        return copies

    def swap_d(step):
        copies = []
        for t in range(2):
            if step == 0:
                three = (total.at[pl.ds((third + 1) * other, third), t], got3.at[t])
                rest = (total.at[third, t, pl.ds(pl.multiple_of(cut * other, 16), mid)], gotm.at[t])
            else:
                three = (put3.at[other, t], new.at[pl.ds((third + 1) * c, third), t])
                rest = (putm.at[other, t], newm.at[t])
            copies.append(send(*three, sem_xs.at[step, t, 0], sem_xr.at[step, t, 0], partner))
            copies.append(send(*rest, sem_xs.at[step, t, 1], sem_xr.at[step, t, 1], partner))
        return copies

    def sums_d():
        copies = []
        for t in range(2):
            for k, (piece, r, row, size) in enumerate(parts(c)):
                for h, src in enumerate((total.at[piece, t, pl.ds(r, size)], got3.at[t, k] if k < third else gotm.at[t])):
                    cols = pl.ds(pl.multiple_of((c, other)[h] * COLS, 128), COLS)
                    copies.append(pltpu.make_async_copy(src, sum_d.at[t, pl.ds(row, size), cols], sem_out.at[t, h, k]))
        return copies

    def step_d():
        for t in range(2):
            for k, (piece, r, row, size) in enumerate(parts(c)):
                for h in range(2):
                    g = (total.at[piece, t, pl.ds(r, size)], got3.at[t, k] if k < third else gotm.at[t])[h]
                    half = (c, other)[h]
                    dst = put3.at[half, t, k] if k < third else putm.at[half, t]
                    for b in range(COLS // 128):
                        lane = pl.ds(pl.multiple_of(half * COLS + 128 * b, 128), 128)
                        here = slice(128 * b, 128 * b + 128)
                        rows = pl.ds(row, size)
                        w = wb3[t, ROWS * k:ROWS * k + ROWS, lane] if k < third else wbm[t, :, lane]
                        adamw(dst.at[:, here], w, mbd[t, rows, lane], vbd[t, rows, lane], g[:, here])

    def merge_d():
        for t in range(2):
            for k in range(third):
                new[(third + 1) * c + k, t] = put3[c, t, k]
            a, b = putm[c, t], newm[t]
            low, high = jnp.where(c == 0, a, b), jnp.where(c == 0, b, a)
            line = lax.broadcasted_iota(jnp.int32, (mid - cut, COLS), 0)
            new[third, t, 0:cut] = low[0:cut]
            new[third, t, cut:mid] = jnp.where(line < top - cut, low[cut:mid].astype(F32), high[0:mid - cut].astype(F32)).astype(BF16)
            new[third, t, mid:ROWS] = high[mid - cut:mid]

    def loads_g(w):
        m, v, weight = ((mg, vg, wg), (mu, vu, wu))[w - 1]
        return [pltpu.make_async_copy(m, mbg, sem_m.at[6]), pltpu.make_async_copy(v, vbg, sem_m.at[7]), pltpu.make_async_copy(weight.at[:, x, y, c], wbg, sem_m.at[8])]

    def sums_g(w):
        out = (sum_g, sum_u)[w - 1]
        return [pltpu.make_async_copy(total.at[w * pieces + p], out.at[:, :, COLS * p:COLS * p + COLS], sem_out.at[p % 2, w - 1, p // 2]) for p in range(pieces)]

    def step_g(w):
        for t in range(2):
            for p in range(pieces):
                for b in range(COLS // 128):
                    here, lane = slice(128 * b, 128 * b + 128), slice(COLS * p + 128 * b, COLS * p + 128 * b + 128)
                    adamw(new.at[w * pieces + p, t, :, here], wbg[t, :, lane], mbg[t, :, lane], vbg[t, :, lane], total[w * pieces + p, t, :, here])

    def block(q, t, i, j):
        a, b = at(t, i, j)
        return whole.at[q, t, c, a, b]

    def line(q, t, i, h=None):
        some = slice(None) if h is None else pl.ds(2 * h, 2)
        return whole.at[q, t, c, i % SIDE, some] if t == 0 else whole.at[q, t, c, some, i % SIDE]

    def across(q, t, i):
        send(line(q, t, i), line(q, t, i), sem_os.at[t], sem_or.at[t], partner).start()

    def gather0(q):
        for t in range(2):
            i, j = place[t]
            for d in range(2):
                send(new.at[q, t], block(q, t, i, j), sem_gs.at[t, d], sem_gr.at[q, t, d], dev_j(t, (1, 3)[d])).start()
            pltpu.make_async_copy(new.at[q, t], block(q, t, i, j), sem_own.at[t, q % 4]).start()

    def gather1(q):
        for t in range(2):
            i, j = place[t]
            wait(new.at[q, t], sem_gr.at[q, t, 0])
            wait(new.at[q, t], sem_gr.at[q, t, 1])
            src = block(q, t, i, j + SIDE - side(q))
            send(src, src, sem_gs.at[t, 2], sem_gr.at[q, t, 2], dev_j(t, side(q))).start()
            wait(new.at[q, t], sem_own.at[t, q % 4])

    def gather2(q):
        for t in range(2):
            i = place[t][0]
            wait(new.at[q, t], sem_gr.at[q, t, 2])
            for d in range(2):
                send(line(q, t, i), line(q, t, i), sem_gs.at[t, 3 + d], sem_gr.at[q, t, 3 + d], dev_i(t, (1, 3)[d])).start()
            across(q, t, i)

    def gather3(q):
        for t in range(2):
            i = place[t][0]
            for d in range(2):
                there = i + (3, 1)[d]
                wait(line(q, t, there), sem_gr.at[q, t, 3 + d])
                send(line(q, t, there, d), line(q, t, there, d), sem_gs.at[t, 5 + d], sem_gr.at[q, t, 5 + d], dev_i(t, (1, 3)[d])).start()
            for d in range(2):
                across(q, t, i + (3, 1)[d])

    def gather4(q):
        for t in range(2):
            i = place[t][0]
            for d in range(2):
                wait(line(q, t, i + 2, d), sem_gr.at[q, t, 5 + d])
            across(q, t, i + 2)

    def when(q, do):
        @pl.when(jnp.logical_and(q >= 0, q < count))
        def _():
            do(q)

    def on(tick, t, do):
        @pl.when(t == tick)
        def _():
            do()

    barrier = pltpu.get_barrier_semaphore()
    peers = [dev(x + 1, y, c), dev(x + 3, y, c), dev(x, y + 1, c), dev(x, y + 3, c), partner]
    for peer in peers:
        pl.semaphore_signal(barrier, inc=1, device_id={"dp": peer}, device_id_type=MESH)
    pl.semaphore_wait(barrier, len(peers))

    for q in range(AHEAD):
        swap(q)
    load(0)
    for copy in loads_d() + loads_g(1):
        copy.start()

    ends = [w * pieces + pieces - 1 + LAG[4] for w in range(WEIGHTS)]
    gathers = ends[0] + 2
    stages = (stage0, stage1, stage2, stage3, stage4)
    rounds = (gather0, gather1, gather2, gather3, gather4)

    def start(copies):
        for copy in copies:
            copy.start()

    def finish(copies):
        for copy in copies:
            copy.wait()

    def d_begin():
        start(swap_d(0))

    def d_step():
        finish(loads_d())
        finish(swap_d(0))
        step_d()
        start(swap_d(1))
        start(sums_d())

    def d_end():
        finish(swap_d(1))
        merge_d()
        finish(sums_d())

    def g_step(w):
        finish(loads_g(w))
        step_g(w)
        if w + 1 < WEIGHTS:
            start(loads_g(w + 1))
        start(sums_g(w))

    def tick(t, _):
        when(t + AHEAD, swap)
        when(t + 1, load)
        for k in range(4, 0, -1):
            when(t - gathers - k, rounds[k])
        for k in range(4, -1, -1):
            when(t - LAG[k], stages[k])
        on(ends[0], t, d_begin)
        on(ends[0] + 1, t, d_step)
        on(ends[0] + 2, t, d_end)
        for w in range(1, WEIGHTS):
            on(ends[w], t, functools.partial(g_step, w))
            on(ends[w] + 1, t, lambda w=w: finish(sums_g(w)))
        when(t - gathers, gather0)
        return 0

    lax.fori_loop(0, count + gathers + 4, tick, 0)

    for z in range(SENT):
        for t in range(2):
            for d in range(2):
                wait(s1.at[z, t, d], sem_s1.at[z, t, d])
                wait(t2.at[z, t, d], sem_t2.at[z, t, d])
                for h in range(2):
                    wait(s2.at[z, t, d, h], sem_s2.at[z, t, d, h])
            wait(t1.at[z, t], sem_t1.at[z, t])
    for t in range(2):
        wait(theirs.at[:, t], sem_swap_s.at[t])
        for k in range(3):
            wait(new.at[:, t], sem_gs.at[t, k])
        for d in range(2):
            wait(whole.at[:, t, c, 0], sem_gs.at[t, 3 + d])
            wait(whole.at[:, t, c, 0, 0:2], sem_gs.at[t, 5 + d])
        wait(whole.at[:, t, c], sem_os.at[t])
        wait(whole.at[:, t, other], sem_or.at[t])


def put(pieces, slots, whole, out_d, out_g, out_u, buf, sem_in, sem_out):
    steps = [(w, t, x) for w in range(WEIGHTS) for t in range(2) for x in range(SIDE)]

    def load(s):
        w, t, x = steps[s]
        return pltpu.make_async_copy(whole.at[w * pieces:w * pieces + pieces, t, :, x], buf.at[s % slots], sem_in.at[s % slots])

    def stores(s):
        w, t, x = steps[s]
        copies = []
        for p in range(pieces):
            for c in range(CORES):
                if w == 0:
                    dst = out_d.at[t, x, :, ROWS * p:ROWS * p + ROWS, COLS * c:COLS * c + COLS]
                else:
                    dst = (out_g, out_u)[w - 1].at[t, x, :, c, :, COLS * p:COLS * p + COLS]
                copies.append(pltpu.make_async_copy(buf.at[s % slots, p, c], dst, sem_out.at[s % slots, p, c]))
        return copies

    ahead = slots // 2
    for s in range(ahead):
        load(s).start()
    for s in range(len(steps)):
        if s + ahead < len(steps):
            if s + ahead >= slots:
                for copy in stores(s + ahead - slots):
                    copy.wait()
            load(s + ahead).start()
        load(s).wait()
        for copy in stores(s):
            copy.start()
    for s in range(max(0, len(steps) - slots), len(steps)):
        for copy in stores(s):
            copy.wait()


def solution(mesh):
    devices = mesh.shape["dp"]
    assert devices == CORES * SIDE * SIDE

    def step(*arrays):
        (gg, gu, gd), (wg, wu, wd), (mg, mu, md), (vg, vu, vd) = (arrays[i : i + 3] for i in (0, 3, 6, 9))
        layers, rows, wide = wg.shape
        tall, narrow = wd.shape[1:]
        pieces = wide // COLS
        chip = tall // (SIDE * SIDE)
        assert layers == 2 and rows == devices * ROWS and narrow == CORES * COLS and chip == pieces * ROWS
        c = lax.axis_index("dp") % CORES
        window = pieces // 2 * ROWS + 24
        extra = window - chip // 2

        def shifted(a):
            return lax.dynamic_update_slice_in_dim(jnp.zeros((layers, window, narrow), F32), a, c * extra, 1)

        split_g = (layers, SIDE, SIDE, CORES, ROWS, wide)
        split_d = (layers, SIDE, SIDE, chip, narrow)
        block = (ROWS, COLS)
        count = WEIGHTS * pieces
        hbm = pl.BlockSpec(memory_space=pltpu.HBM)
        dma = pltpu.SemaphoreType.DMA
        third, mid = pieces // 2, 24
        whole, sum_d, sum_g, sum_u, _ = pl.pallas_call(
            functools.partial(fused, pieces),
            out_shape=(
                jax.ShapeDtypeStruct((count, 2, CORES, SIDE, SIDE, *block), BF16),
                jax.ShapeDtypeStruct((layers, window, narrow), BF16),
                jax.ShapeDtypeStruct((layers, ROWS, wide), BF16),
                jax.ShapeDtypeStruct((layers, ROWS, wide), BF16),
                jax.ShapeDtypeStruct((count, 2, SIDE, SIDE, *block), BF16),
            ),
            in_specs=[hbm] * 12,
            out_specs=[hbm] * 5,
            scratch_shapes=[
                pltpu.VMEM((HELD, 2, SIDE, SIDE, *block), BF16),
                pltpu.VMEM((HELD, 2, SIDE, SIDE, *block), BF16),
                pltpu.VMEM((SLOTS, 2, 2, 2, *block), BF16),
                pltpu.VMEM((SLOTS, 2, 2, 2, 2, *block), BF16),
                pltpu.VMEM((SLOTS, 2, *block), BF16),
                pltpu.VMEM((SLOTS, 2, 2, *block), BF16),
                pltpu.VMEM((SENT, 2, 2, 2, *block), BF16),
                pltpu.VMEM((SENT, 2, 2, 2, 2, *block), BF16),
                pltpu.VMEM((SENT, 2, *block), BF16),
                pltpu.VMEM((SENT, 2, 2, *block), BF16),
                pltpu.VMEM((count, 2, *block), BF16),
                pltpu.VMEM((count, 2, *block), BF16),
                pltpu.VMEM((2, third, *block), BF16),
                pltpu.VMEM((2, mid, COLS), BF16),
                pltpu.VMEM((CORES, 2, third, *block), BF16),
                pltpu.VMEM((CORES, 2, mid, COLS), BF16),
                pltpu.VMEM((2, mid, COLS), BF16),
                pltpu.VMEM((layers, window, narrow), F32),
                pltpu.VMEM((layers, window, narrow), F32),
                pltpu.VMEM((layers, third * ROWS, narrow), BF16),
                pltpu.VMEM((layers, mid, narrow), BF16),
                pltpu.VMEM((layers, ROWS, wide), F32),
                pltpu.VMEM((layers, ROWS, wide), F32),
                pltpu.VMEM((layers, ROWS, wide), BF16),
                dma((2, 2, 2)),
                dma((2,)),
                dma((count, 2)),
                dma((SLOTS, 2, 2)),
                dma((SLOTS, 2, 2, 2)),
                dma((SLOTS, 2)),
                dma((SLOTS, 2, 2)),
                dma((SENT, 2, 2)),
                dma((SENT, 2, 2, 2)),
                dma((SENT, 2)),
                dma((SENT, 2, 2)),
                dma((9,)),
                dma((2, 2, 4)),
                dma((2, 2, 2)),
                dma((2, 2, 2)),
                dma((2, 4)),
                dma((2, 7)),
                dma((count, 2, 7)),
                dma((2,)),
                dma((2,)),
            ],
            name="fused",
            compiler_params=pltpu.CompilerParams(collective_id=0, has_side_effects=True, vmem_limit_bytes=62 * 2**20),
        )(
            gd.reshape(split_d), gg.reshape(split_g), gu.reshape(split_g), wd.reshape(split_d), wg.reshape(split_g), wu.reshape(split_g),
            shifted(md), shifted(vd), mg, vg, mu, vu,
        )
        slots = 12
        new_d, new_g, new_u = pl.pallas_call(
            functools.partial(put, pieces, slots),
            out_shape=tuple(jax.ShapeDtypeStruct(s, BF16) for s in (split_d, split_g, split_g)),
            in_specs=[hbm],
            out_specs=[hbm] * 3,
            scratch_shapes=[pltpu.VMEM((slots, pieces, CORES, SIDE, *block), BF16), dma((slots,)), dma((slots, pieces, CORES))],
            name="put",
            compiler_params=pltpu.CompilerParams(vmem_limit_bytes=62 * 2**20),
        )(whole)
        g = (sum_g, sum_u, lax.dynamic_slice_in_dim(sum_d, c * extra, chip // 2, 1))
        g = [one.astype(F32) for one in g]
        m = [0.9 * a + 0.1 * b for a, b in zip((mg, mu, md), g)]
        v = [0.95 * a + 0.05 * b * b for a, b in zip((vg, vu, vd), g)]
        return (new_g.reshape(wg.shape), new_u.reshape(wu.shape), new_d.reshape(wd.shape), *m, *v)

    all_of, cut = P(None, None, None), P(None, "dp", None)
    return jax.shard_map(
        step,
        mesh=mesh,
        in_specs=(P(("rep", "dp"), None, None, None),) * 3 + (all_of,) * 3 + (cut,) * 6,
        out_specs=(P("rep", None, None),) * 3 + (P("rep", "dp", None),) * 6,
        check_vma=False,
    )
```

time: 848 us -> 451 us (0.53)
  waiting for transfers between devices: 440 us -> 0 us
  Pallas kernels: 0 us -> 423 us
  local copies, waits for them, and re-layouts: 379 us -> 22 us
  between operations: 14.2 us -> 0.8 us
  other arithmetic: 14.5 us -> 5.16 us
    pallas_call x0 -> x2, Pallas kernels: none -> 423 us  [the longest x1 377 us: step(): pl.pallas_call(functools.partial(fused, pieces), out_shape=(jax.ShapeDtyp...]
    unnamed x18 -> x24, local copies, waits for them, and re-layouts: 378 us -> 9.64 us
    all_gather x3 -> x0, waiting for transfers between devices: 222 us -> none  [step(): whole = [lax.all_gather(one[0], 'dp', axis=1, tiled=True) for one in new]]
    unnamed x9 -> x0, waiting for transfers between devices: 218 us -> none
    convert_element_type x3 -> x0, other arithmetic: 14.5 us -> none  [adamw(): return ((w - 0.02 * step).astype(jnp.bfloat16), m, v)]
    dynamic_update_slice x0 -> x2, local copies, waits for them, and re-layouts: none -> 12.1 us  [shifted(): lax.dynamic_update_slice_in_dim(jnp.zeros((layers, window, narrow), F32),...]
  transfers between devices with their start and end apart: 6 -> 0, of which waited for: 5 -> 0; matrix products, arithmetic and copies ran while one was open for 30% -> 0% of each run, Pallas kernels for 0% -> 0%
where the time goes in v1:
time: 451 us
  Pallas kernels  423 us (94%)
  local copies, waits for them, and re-layouts  22 us (5%)
  other arithmetic  5.16 us (1%)
    pallas_call x1, Pallas kernels, step(): pl.pallas_call(functools.partial(fused, pieces), out_shape=(jax.ShapeDtyp...  377 us
    pallas_call x1, Pallas kernels, step(): pl.pallas_call(functools.partial(put, pieces, slots), out_shape=tuple((ja...  46.3 us
    dynamic_update_slice x2, local copies, waits for them, and re-layouts, shifted(): lax.dynamic_update_slice_in_dim(jnp.zeros((layers, window, narrow), F32),...  12.1 us
    unnamed x24, local copies, waits for them, and re-layouts  9.64 us

profile of v1, /device:TPU:97, one launch (start us, length us, event | category | flops | bytes accessed | tf_op | source)
XLA Modules:
  0.0 450.9 jit_solution(17127101921191218440)
XLA Ops:
  0.7 0.0 copy-start.7
  0.7 1.6 copy.21
  2.2 0.2 copy-done.7
  2.5 1.2 copy.22
  3.7 0.1 broadcast.16.clone
  3.8 5.7 %dynamic_update_slice.6.refs_6_ = f32[2,144,1280]{2,1,0:T(8,128)S(1)} dynamic-update-slice(f32[2,144,1280]{2,1,0:T(8,128)S(1)} %broadcast.16.clone, f32[2,140,1280]{2,1,0:T(8,128)S(1)} %copy.21, s32[]{:T(128)} %constant.12.clone.1, s32[]{:T(128)S(6)} %select_n.13, s32[]{:T(128)} %constant.12.clone.1) | dynamic-update-slice | bytes 2867204 | tf_op jit(solution)/shard_map/dynamic_update_slice | solution.py:467
  9.5 0.0 copy-start.1
  9.5 1.1 copy-done.1
  10.6 0.1 broadcast.16.clone.1
  10.7 6.4 %dynamic_update_slice.7.refs_7_ = f32[2,144,1280]{2,1,0:T(8,128)S(1)} dynamic-update-slice(f32[2,144,1280]{2,1,0:T(8,128)S(1)} %broadcast.16.clone.1, f32[2,140,1280]{2,1,0:T(8,128)} %copy.22, s32[]{:T(128)} %constant.12.clone.1, s32[]{:T(128)S(6)} %select_n.13, s32[]{:T(128)} %constant.12.clone.1) | dynamic-update-slice | bytes 2867204 | tf_op jit(solution)/shard_map/dynamic_update_slice | solution.py:467
  17.1 0.0 copy-start
  17.1 1.1 copy-done
  18.2 376.7 %fused.1 = (bf16[21,2,2,4,4,40,640]{6,5,4,3,2,1,0:T(8,128)(2,1)}, bf16[2,144,1280]{2,1,0:T(8,128)(2,1)}, bf16[2,40,4480]{2,1,0:T(8,128)(2,1)}, bf16[2,40,4480]{2...) custom-call(bf16[2,4,4,280,1280]{4,3,2,1,0:T(8,128)(2,1)} %bitcast.9, bf16[2,4,4,2,40,4480]{5,4,3,2,1,0:T(8,128)(2,1)} %bitcast.10, ...), custom_call_target="tpu_custom_call" | custom-call | tf_op jit(solution)/shard_map/fused/pallas_call | solution.py:476
  394.9 0.0 copy-start.6
  395.0 46.3 %put.1 = (bf16[2,4,4,280,1280]{4,3,2,1,0:T(8,128)(2,1)}, bf16[2,4,4,2,40,4480]{5,4,3,2,1,0:T(8,128)(2,1)}, bf16[2,4,4,2,40,4480]{5,4,3,2,1,0:T(8,128)(2,1)}) custom-call(bf16[21,2,2,4,4,40,640]{6,5,4,3,2,1,0:T(8,128)(2,1)} %get-tuple-element.16.whole), custom_call_target="tpu_custom_call" | custom-call | tf_op jit(solution)/shard_map/put/pallas_call | solution.py:540
  441.2 0.0 copy-done.6
  441.3 0.0 copy-start.8
  441.3 0.0 copy-start.9
  441.3 2.2 fusion.1
  443.5 0.0 copy-start.4
  443.5 0.0 copy-start.5
  443.5 2.2 copy.26
  445.7 0.0 copy-start.2
  445.7 0.0 copy-start.3
  445.7 2.2 copy.25
  447.9 0.0 copy-done.8
  447.9 0.0 copy-done.9
  447.9 0.0 copy-done.4
  447.9 0.0 copy-done.5
  447.9 0.0 copy-done.2
  448.0 0.0 copy-done.3
  448.0 2.9 fusion.4
Async XLA Ops:
  0.7 1.8 copy-start.7
  9.5 1.1 copy-start.1
  17.1 1.1 copy-start
  394.9 46.3 %copy-start.6 = (f32[2,140,1280]{2,0,1:T(2,128)S(1)}, f32[2,140,1280]{2,0,1:T(2,128)}, u32[]{:S(2)}) copy-start(f32[2,140,1280]{2,0,1:T(2,128)} %param.20) | copy-start | bytes 4300804
  441.3 6.7 %copy-start.8 = (bf16[2,40,4480]{2,1,0:T(8,128)(2,1)S(1)}, bf16[2,40,4480]{2,1,0:T(8,128)(2,1)}, u32[]{:S(2)}) copy-start(bf16[2,40,4480]{2,1,0:T(8,128)(2,1)} %get-tuple-element.20) | copy-start | bytes 2150404
  441.3 6.7 %copy-start.9 = (bf16[2,40,4480]{2,1,0:T(8,128)(2,1)S(1)}, bf16[2,40,4480]{2,1,0:T(8,128)(2,1)}, u32[]{:S(2)}) copy-start(bf16[2,40,4480]{2,1,0:T(8,128)(2,1)} %get-tuple-element.21) | copy-start | bytes 2150404
  443.5 4.4 copy-start.4
  443.5 4.4 copy-start.5
  445.7 2.2 copy-start.2
  445.7 2.2 copy-start.3

commit v2 on v1

v2 whole, which is shorter than its diff:
```python
import functools
import math

import jax
import jax.numpy as jnp
from jax import lax
from jax.experimental import pallas as pl
from jax.experimental.pallas import tpu as pltpu
from jax.sharding import PartitionSpec as P

MESH = pl.DeviceIdType.MESH
F32, BF16 = jnp.float32, jnp.bfloat16
CORES, SIDE = 2, 4
WEIGHTS = 3
ROWS, COLS = 40, 640
LAG = (0, 1, 2, 3, 4)
ROUND = (0, 2, 4, 6, 8, 9)
SLOTS = LAG[4] + LAG[2] + 2
HELD = LAG[4] + 2
SENT = 3
AHEAD = 3
FROM, TO = 6, 20


def fused(pieces, *refs):
    (gd, gg, gu, wd, wg, wu, md, vd, mg, vg, mu, vu, whole, kept, theirs, mbd, vbd, mbg, vbg, mbu, vbu,
     total, new, got3, gotm, put3, putm, newm, wb3, wbm, wbg,
     sem_load, sem_first, sem_swap_s, sem_swap_r, sem_r1, sem_r2, sem_u1, sem_u2, sem_s1, sem_s2, sem_t1, sem_t2,
     sem_m, sem_xs, sem_xr, sem_own, sem_gs, sem_gr, sem_os, sem_or, sem_kept) = refs
    count = WEIGHTS * pieces
    me = lax.axis_index("dp")
    x, y, c = me // (CORES * SIDE), (me // CORES) % SIDE, me % CORES
    other = 1 - c

    def dev(x, y, c):
        return ((x % SIDE) * SIDE + y % SIDE) * CORES + c

    partner = dev(x, y, other)
    place = ((x, y), (y, x))

    def dev_i(t, d):
        return dev(x + d, y, c) if t == 0 else dev(x, y + d, c)

    def dev_j(t, d):
        return dev_i(1 - t, d)

    def at(t, i, j):
        return (i % SIDE, j % SIDE) if t == 0 else (j % SIDE, i % SIDE)

    def send(src, dst, ssem, rsem, to):
        return pltpu.make_async_remote_copy(src_ref=src, dst_ref=dst, send_sem=ssem, recv_sem=rsem, device_id={"dp": to}, device_id_type=MESH)

    def wait(ref, sem):
        pltpu.make_async_copy(ref, ref, sem).wait()

    def own(q, t):
        return kept.at[q % HELD, t, 0]

    def par(q, t):
        return kept.at[q % HELD, t, 1]

    def r1(q, t, d):
        r = q % SLOTS
        return kept.at[HELD, t, d, r // 2, pl.ds(r % 2 * 2, 2)]

    def r2(q, t, d, h):
        r = q % SLOTS
        return kept.at[HELD + 1 + h, t, d, r // 2, pl.ds(r % 2 * 2, 2)]

    def u1(q, t):
        r = q % SLOTS
        return kept.at[HELD + 3, t, 0, 2 + r // SIDE, r % SIDE]

    def u2(q, t, e):
        r = q % SLOTS
        return kept.at[HELD + 3, t, e, r // SIDE, r % SIDE]

    def s1(q, t, d):
        return kept.at[HELD + 4, t, d, q % SENT, pl.ds(0, 2)]

    def s2(q, t, d, h):
        return kept.at[HELD + 5, t, d, q % SENT, pl.ds(2 * h, 2)]

    def t1(q, t):
        return kept.at[HELD + 4, t, 0, q % SENT, 2]

    def t2(q, t, e):
        return kept.at[HELD + 4, t, e, q % SENT, 3]

    def of_weight(q, do):
        for w in range(WEIGHTS):
            @pl.when(q // pieces == w)
            def _(w=w):
                do(w, q % pieces)

    def term(w, t, p, core):
        if w == 0:
            return gd.at[t, :, :, pl.ds(pl.multiple_of(p * ROWS, 8), ROWS), pl.ds(pl.multiple_of(core * COLS, 128), COLS)]
        return (gg, gu)[w - 1].at[t, :, :, core, :, pl.ds(pl.multiple_of(p * COLS, 128), COLS)]

    def swap(q):
        def do(w, p):
            for t in range(2):
                send(term(w, t, p, other), theirs.at[q, t], sem_swap_s.at[t], sem_swap_r.at[q, t], partner).start()
        of_weight(q, do)

    def load_own(q):
        def do(w, p):
            for t in range(2):
                pltpu.make_async_copy(term(w, t, p, c), own(q, t), sem_load.at[0, t, q % 2]).start()
        of_weight(q, do)

    def load(q):
        load_own(q)
        for t in range(2):
            wait(theirs.at[q, t], sem_swap_r.at[q, t])
            pltpu.make_async_copy(theirs.at[q, t], par(q, t), sem_load.at[1, t, q % 2]).start()

    def add(dst, *srcs):
        for k in range(COLS // 128):
            cut = (slice(None), slice(128 * k, 128 * k + 128))
            value = srcs[0][cut].astype(F32)
            for src in srcs[1:]:
                value = value + src[cut].astype(F32)
            dst[cut] = value.astype(dst.dtype)

    def both(q, t, i, j):
        a, b = at(t, i, j)
        return own(q, t).at[a, b], par(q, t).at[a, b]

    def freed(buf, sem, q):
        @pl.when(q >= SENT)
        def _():
            wait(buf, sem)

    def first(q, t, d):
        return send(s1(q, t, d), r1(q, t, d), sem_s1.at[q % SENT, t, d], sem_r1.at[q % SLOTS, t, d], dev_i(t, (1, 3)[d]))

    def second(q, t, d, h):
        return send(s2(q, t, d, h), r2(q, t, d, h), sem_s2.at[q % SENT, t, d, h], sem_r2.at[q % SLOTS, t, d, h], dev_i(t, (1, 3)[d]))

    def far_chunk(q, t):
        for d in range(2):
            for b in range(2):
                add(s1(q, t, d).at[b], *both(q, t, place[t][0] + 2, 2 * d + b))
        for d in range(2):
            first(q, t, d).start()

    def near_chunks(q, t):
        for d in range(2):
            for b in range(2):
                add(s2(q, t, d, 1 - d).at[b], *both(q, t, place[t][0] + (1, 3)[d], 2 * (1 - d) + b))
        for d in range(2):
            second(q, t, d, 1 - d).start()

    def chunk(t, k):
        def of(ref):
            i = (place[t][0] + (2, 1, 3, 0)[k]) % SIDE
            return ref.at[i] if t == 0 else ref.at[:, i]
        return send(of(term(0, t, 0, other)), of(par(0, t)), sem_first.at[0, t, k], sem_first.at[1, t, k], partner)

    def stage0_first():
        for t in range(2):
            wait(own(0, t), sem_load.at[0, t, 0])
            chunk(t, 0).wait_recv()
            far_chunk(0, t)
        for t in range(2):
            for k in range(1, 3):
                chunk(t, k).wait_recv()
            near_chunks(0, t)
        for t in range(2):
            chunk(t, 3).wait_recv()
            for k in range(4):
                chunk(t, k).wait_send()

    def stage0(q):
        for t in range(2):
            wait(own(q, t), sem_load.at[0, t, q % 2])
            wait(par(q, t), sem_load.at[1, t, q % 2])
        for t in range(2):
            for d in range(2):
                freed(s1(q, t, d), sem_s1.at[q % SENT, t, d], q)
            far_chunk(q, t)
        for t in range(2):
            for d in range(2):
                freed(s2(q, t, d, 1 - d), sem_s2.at[q % SENT, t, d, 1 - d], q)
            near_chunks(q, t)

    def stage1(q):
        for t in range(2):
            for d in range(2):
                freed(s2(q, t, d, d), sem_s2.at[q % SENT, t, d, d], q)
                wait(r1(q, t, d), sem_r1.at[q % SLOTS, t, d])
                for b in range(2):
                    add(s2(q, t, d, d).at[b], r1(q, t, d).at[b], *both(q, t, place[t][0] + (1, 3)[d], 2 * d + b))
            for d in range(2):
                second(q, t, d, d).start()

    def cell(q, t, j):
        j = j % SIDE
        came = [kept.at[HELD + 1 + j // 2, t, d, q % SLOTS // 2, q % SLOTS % 2 * 2 + j % 2] for d in range(2)]
        return (*came, *both(q, t, place[t][0], j))

    def side(q):
        return 1 + 2 * (q % 2)

    def far(q, t):
        return send(t1(q, t), u1(q, t), sem_t1.at[q % SENT, t], sem_u1.at[q % SLOTS, t], dev_j(t, side(q)))

    def near(q, t, e):
        to = (side(q), SIDE - side(q))[e]
        return send(t2(q, t, e), u2(q, t, e), sem_t2.at[q % SENT, t, e], sem_u2.at[q % SLOTS, t, e], dev_j(t, to))

    def stage2(q):
        for t in range(2):
            j = place[t][1]
            for d in range(2):
                for h in range(2):
                    wait(r2(q, t, d, h), sem_r2.at[q % SLOTS, t, d, h])
            freed(t1(q, t), sem_t1.at[q % SENT, t], q)
            freed(t2(q, t, 1), sem_t2.at[q % SENT, t, 1], q)
            add(t1(q, t), *cell(q, t, j + 2))
            add(t2(q, t, 1), *cell(q, t, j + SIDE - side(q)))
            far(q, t).start()
            near(q, t, 1).start()

    def stage3(q):
        for t in range(2):
            freed(t2(q, t, 0), sem_t2.at[q % SENT, t, 0], q)
            wait(u1(q, t), sem_u1.at[q % SLOTS, t])
            add(t2(q, t, 0), u1(q, t), *cell(q, t, place[t][1] + side(q)))
            near(q, t, 0).start()

    def stage4(q):
        for t in range(2):
            for e in range(2):
                wait(u2(q, t, e), sem_u2.at[q % SLOTS, t, e])
            add(total.at[q, t], u2(q, t, 0), u2(q, t, 1), *cell(q, t, place[t][1]))

    def adamw(dst, w, m, v, g):
        w, g = w.astype(F32), g.astype(F32)
        m = 0.9 * m + 0.1 * g
        v = 0.95 * v + 0.05 * g * g
        step = m * lax.rsqrt(v + 1e-8) + 0.1 * w
        dst[...] = (w - 0.02 * step).astype(BF16)
        return m, v

    third, mid = pieces // 2, 24
    top, cut = pieces * ROWS // 2 - third * ROWS, 16

    def parts(core):
        return [((third + 1) * core + k, 0, pl.multiple_of(mid * core + ROWS * k, 8), ROWS) for k in range(third)] + [
            (third, pl.multiple_of(cut * core, 16), pl.multiple_of(third * ROWS * (1 - core), 8), mid)]

    mine = pl.ds((mid + third * ROWS - md.shape[0]) * c, md.shape[0])

    def loads_d():
        copies = [pltpu.make_async_copy(md, mbd.at[mine], sem_m.at[0, 0]), pltpu.make_async_copy(vd, vbd.at[mine], sem_m.at[1, 0])]
        rows = pl.ds(pl.multiple_of((third + 1) * ROWS * c, 8), third * ROWS)
        for t in range(2):
            copies.append(pltpu.make_async_copy(wd.at[t, x, y, rows], wb3.at[t], sem_m.at[2 + t, 0]))
            rest = pl.ds(pl.multiple_of(third * ROWS + cut * c, 8), mid)
            copies.append(pltpu.make_async_copy(wd.at[t, x, y, rest], wbm.at[t], sem_m.at[4 + t, 0]))
        return copies

    def swap_d(step):
        copies = []
        for t in range(2):
            if step == 0:
                three = (total.at[pl.ds((third + 1) * other, third), t], got3.at[t])
                rest = (total.at[third, t, pl.ds(pl.multiple_of(cut * other, 16), mid)], gotm.at[t])
            else:
                three = (put3.at[other, t], new.at[pl.ds((third + 1) * c, third), t])
                rest = (putm.at[other, t], newm.at[t])
            copies.append(send(*three, sem_xs.at[step, t, 0], sem_xr.at[step, t, 0], partner))
            copies.append(send(*rest, sem_xs.at[step, t, 1], sem_xr.at[step, t, 1], partner))
        return copies

    def step_d():
        for t in range(2):
            for k, (piece, r, row, size) in enumerate(parts(c)):
                for h in range(2):
                    g = (total.at[piece, t, pl.ds(r, size)], got3.at[t, k] if k < third else gotm.at[t])[h]
                    half = (c, other)[h]
                    dst = put3.at[half, t, k] if k < third else putm.at[half, t]
                    for b in range(COLS // 128):
                        lane = pl.ds(pl.multiple_of(half * COLS + 128 * b, 128), 128)
                        here = slice(128 * b, 128 * b + 128)
                        rows = pl.ds(row, size)
                        w = wb3[t, ROWS * k:ROWS * k + ROWS, lane] if k < third else wbm[t, :, lane]
                        mbd[rows, t, lane], vbd[rows, t, lane] = adamw(dst.at[:, here], w, mbd[rows, t, lane], vbd[rows, t, lane], g[:, here])

    def merge_d():
        for t in range(2):
            for k in range(third):
                new[(third + 1) * c + k, t] = put3[c, t, k]
            a, b = putm[c, t], newm[t]
            low, high = jnp.where(c == 0, a, b), jnp.where(c == 0, b, a)
            line = lax.broadcasted_iota(jnp.int32, (mid - cut, COLS), 0)
            new[third, t, 0:cut] = low[0:cut]
            new[third, t, cut:mid] = jnp.where(line < top - cut, low[cut:mid].astype(F32), high[0:mid - cut].astype(F32)).astype(BF16)
            new[third, t, mid:ROWS] = high[mid - cut:mid]

    def loads_g(w):
        (m, v), (mb, vb) = (((mg, vg), (mbg, vbg)), ((mu, vu), (mbu, vbu)))[w - 1]
        return [pltpu.make_async_copy(m, mb, sem_m.at[6, w - 1]), pltpu.make_async_copy(v, vb, sem_m.at[7, w - 1])]

    def load_w(w):
        return pltpu.make_async_copy((wg, wu)[w - 1].at[:, x, y, c], wbg, sem_m.at[8, w - 1])

    def step_g(w):
        mb, vb = ((mbg, vbg), (mbu, vbu))[w - 1]
        for t in range(2):
            for p in range(pieces):
                for b in range(COLS // 128):
                    here, lane = slice(128 * b, 128 * b + 128), slice(COLS * p + 128 * b, COLS * p + 128 * b + 128)
                    mb[t, :, lane], vb[t, :, lane] = adamw(
                        new.at[w * pieces + p, t, :, here], wbg[t, :, lane], mb[t, :, lane], vb[t, :, lane], total[w * pieces + p, t, :, here])

    def block(q, t, i, j):
        a, b = at(t, i, j)
        return whole.at[q, t, c, a, b]

    def line(q, t, i, h=None):
        some = slice(None) if h is None else pl.ds(2 * h, 2)
        return whole.at[q, t, c, i % SIDE, some] if t == 0 else whole.at[q, t, c, some, i % SIDE]

    def across(q, t, i):
        send(line(q, t, i), line(q, t, i), sem_os.at[t], sem_or.at[q, t], partner).start()

    def gather0(q):
        for t in range(2):
            i, j = place[t]
            for d in range(2):
                send(new.at[q, t], block(q, t, i, j), sem_gs.at[t, d], sem_gr.at[q, t, d], dev_j(t, (1, 3)[d])).start()
            pltpu.make_async_copy(new.at[q, t], block(q, t, i, j), sem_own.at[t, q % 4]).start()

    def gather1(q):
        for t in range(2):
            i, j = place[t]
            wait(new.at[q, t], sem_gr.at[q, t, 0])
            wait(new.at[q, t], sem_gr.at[q, t, 1])
            src = block(q, t, i, j + SIDE - side(q))
            send(src, src, sem_gs.at[t, 2], sem_gr.at[q, t, 2], dev_j(t, side(q))).start()
            wait(new.at[q, t], sem_own.at[t, q % 4])

    def gather2(q):
        for t in range(2):
            i = place[t][0]
            wait(new.at[q, t], sem_gr.at[q, t, 2])
            for k in range(2):
                for d in range(2):
                    half = line(q, t, i, (d, 1 - d)[k])
                    send(half, half, sem_gs.at[t, 3 + 2 * k + d], sem_gr.at[q, t, 3 + 2 * k + d], dev_i(t, (1, 3)[d])).start()
            across(q, t, i)

    def gather3(q):
        for t in range(2):
            for d in range(2):
                half = line(q, t, place[t][0] + (3, 1)[d], d)
                wait(half, sem_gr.at[q, t, 3 + d])
                send(half, half, sem_gs.at[t, 7 + d], sem_gr.at[q, t, 7 + d], dev_i(t, (1, 3)[d])).start()
        for t in range(2):
            for d in range(2):
                there = place[t][0] + (3, 1)[d]
                wait(line(q, t, there, 1 - d), sem_gr.at[q, t, 5 + d])
                across(q, t, there)

    def gather4(q):
        for t in range(2):
            i = place[t][0]
            for d in range(2):
                wait(line(q, t, i + 2, d), sem_gr.at[q, t, 7 + d])
            across(q, t, i + 2)

    def keep(q):
        for t in range(2):
            wait(whole.at[q, t, other], sem_or.at[q, t])

        @pl.when(jnp.logical_and(q >= FROM, q < TO))
        def _():
            pltpu.make_async_copy(whole.at[q], kept.at[q - FROM], sem_kept).start()

    def when(q, do):
        @pl.when(jnp.logical_and(q >= 0, q < count))
        def _():
            do(q)

    def on(tick, t, do):
        @pl.when(t == tick)
        def _():
            do()

    load_own(0)
    barrier = pltpu.get_barrier_semaphore()
    peers = [dev(x + 1, y, c), dev(x + 3, y, c), dev(x, y + 1, c), dev(x, y + 3, c), partner]
    for peer in peers:
        pl.semaphore_signal(barrier, inc=1, device_id={"dp": peer}, device_id_type=MESH)
    pl.semaphore_wait(barrier, len(peers))
    for k in range(4):
        for t in range(2):
            chunk(t, k).start()
    for q in range(1, AHEAD):
        swap(q)
    for copy in loads_d() + loads_g(1) + loads_g(2) + [load_w(1)]:
        copy.start()
    stage0_first()

    ends = [w * pieces + pieces - 1 + LAG[4] for w in range(WEIGHTS)]
    gathers = ends[0] + 2
    stages = (stage0, stage1, stage2, stage3, stage4)
    rounds = (gather0, gather1, gather2, gather3, gather4, keep)
    assert FROM + gathers + ROUND[5] > ends[-1] + 1 and TO - FROM == kept.shape[0] and HELD + 6 <= TO - FROM

    def start(copies):
        for copy in copies:
            copy.start()

    def finish(copies):
        for copy in copies:
            copy.wait()

    def d_begin():
        start(swap_d(0))

    def d_step():
        finish(loads_d())
        finish(swap_d(0))
        step_d()
        start(swap_d(1))

    def d_end():
        finish(swap_d(1))
        merge_d()

    def g_step(w):
        finish(loads_g(w))
        load_w(w).wait()
        step_g(w)
        if w + 1 < WEIGHTS:
            load_w(w + 1).start()

    def sent():
        for z in range(SENT):
            for t in range(2):
                for d in range(2):
                    wait(s1(z, t, d), sem_s1.at[z, t, d])
                    wait(t2(z, t, d), sem_t2.at[z, t, d])
                    for h in range(2):
                        wait(s2(z, t, d, h), sem_s2.at[z, t, d, h])
                wait(t1(z, t), sem_t1.at[z, t])

    def tick(t, _):
        when(t + AHEAD, swap)
        when(t + 1, load)
        for k in range(5, 0, -1):
            when(t - gathers - ROUND[k], rounds[k])
        for k in range(4, 0, -1):
            when(t - LAG[k], stages[k])

        @pl.when(t > 0)
        def _():
            when(t, stage0)
        on(ends[0], t, d_begin)
        on(ends[0] + 1, t, d_step)
        on(ends[0] + 2, t, d_end)
        for w in range(1, WEIGHTS):
            on(ends[w], t, functools.partial(g_step, w))
        on(ends[-1] + 1, t, sent)
        when(t - gathers, gather0)
        return 0

    lax.fori_loop(0, count + gathers + ROUND[5], tick, 0)

    for t in range(2):
        wait(theirs.at[1:, t], sem_swap_s.at[t])
        for k in range(3):
            wait(new.at[:, t], sem_gs.at[t, k])
        for d in range(2):
            for k in range(3):
                wait(whole.at[:, t, c, 0, 0:2], sem_gs.at[t, 3 + 2 * k + d])
        wait(whole.at[:, t, c], sem_os.at[t])
    wait(kept, sem_kept)


def put(pieces, slots, whole, kept, mbd, vbd, mbg, vbg, mbu, vbu, out_d, out_g, out_u, md, vd, mg, vg, mu, vu, buf, sem_in, sem_out, sem_kept, sem_m):
    steps = [(q, t) for q in range(WEIGHTS * pieces) for t in range(2) if not FROM <= q < TO]
    rest = [(q, t) for q in range(FROM, TO) for t in range(2)]

    def dst(q, t, c):
        w, p = divmod(q, pieces)
        if w == 0:
            return out_d.at[t, :, :, ROWS * p:ROWS * p + ROWS, COLS * c:COLS * c + COLS]
        return (out_g, out_u)[w - 1].at[t, :, :, c, :, COLS * p:COLS * p + COLS]

    def load(s):
        q, t = steps[s]
        return pltpu.make_async_copy(whole.at[q, t], buf.at[s % slots], sem_in.at[s % slots])

    def stores(s):
        return [pltpu.make_async_copy(buf.at[s % slots, c], dst(*steps[s], c), sem_out.at[s % slots, c]) for c in range(CORES)]

    mine = pl.ds((mbd.shape[0] - md.shape[0]) * (lax.axis_index("dp") % CORES), md.shape[0])
    moments = [(mbd.at[mine], md), (vbd.at[mine], vd), (mbg, mg), (vbg, vg), (mbu, mu), (vbu, vu)]
    moments = [pltpu.make_async_copy(src, dst, sem_m.at[k]) for k, (src, dst) in enumerate(moments)]
    ahead = slots // 2
    for s in range(ahead):
        load(s).start()
    for copy in moments:
        copy.start()
    for s in range(len(steps)):
        for q, t in rest[len(rest) * s // len(steps):len(rest) * (s + 1) // len(steps)]:
            for c in range(CORES):
                pltpu.make_async_copy(kept.at[q - FROM, t, c], dst(q, t, c), sem_kept).start()
        if s + ahead < len(steps):
            if s + ahead >= slots:
                for copy in stores(s + ahead - slots):
                    copy.wait()
            load(s + ahead).start()
        load(s).wait()
        for copy in stores(s):
            copy.start()
    for s in range(max(0, len(steps) - slots), len(steps)):
        for copy in stores(s):
            copy.wait()
    pltpu.make_async_copy(kept, kept, sem_kept).wait()
    for copy in moments:
        copy.wait()


def solution(mesh):
    devices = mesh.shape["dp"]
    assert devices == CORES * SIDE * SIDE

    def step(*arrays):
        (gg, gu, gd), (wg, wu, wd), (mg, mu, md), (vg, vu, vd) = (arrays[i : i + 3] for i in (0, 3, 6, 9))
        layers, rows, wide = wg.shape
        tall, narrow = wd.shape[1:]
        pieces = wide // COLS
        chip = tall // (SIDE * SIDE)
        assert layers == 2 and rows == devices * ROWS and narrow == CORES * COLS and chip == pieces * ROWS
        split_g = (layers, SIDE, SIDE, CORES, ROWS, wide)
        split_d = (layers, SIDE, SIDE, chip, narrow)
        block = (ROWS, COLS)
        count = WEIGHTS * pieces
        hbm, vmem = pl.BlockSpec(memory_space=pltpu.HBM), pl.BlockSpec(memory_space=pltpu.VMEM)
        dma = pltpu.SemaphoreType.DMA
        third, mid = pieces // 2, 24
        window = third * ROWS + mid
        md, vd = (a.transpose(1, 0, 2) for a in (md, vd))
        whole, kept, _, *moments = pl.pallas_call(
            functools.partial(fused, pieces),
            out_shape=(
                jax.ShapeDtypeStruct((count, 2, CORES, SIDE, SIDE, *block), BF16),
                pltpu.VMEM((TO - FROM, 2, CORES, SIDE, SIDE, *block), BF16),
                jax.ShapeDtypeStruct((count, 2, SIDE, SIDE, *block), BF16),
                *(pltpu.VMEM((window, *md.shape[1:]), F32) for _ in range(2)),
                *(pltpu.VMEM(mg.shape, F32) for _ in range(4)),
            ),
            in_specs=[hbm] * 12,
            out_specs=[hbm, vmem, hbm] + [vmem] * 6,
            scratch_shapes=[
                pltpu.VMEM((count, 2, *block), BF16),
                pltpu.VMEM((count, 2, *block), BF16),
                pltpu.VMEM((2, third, *block), BF16),
                pltpu.VMEM((2, mid, COLS), BF16),
                pltpu.VMEM((CORES, 2, third, *block), BF16),
                pltpu.VMEM((CORES, 2, mid, COLS), BF16),
                pltpu.VMEM((2, mid, COLS), BF16),
                pltpu.VMEM((layers, third * ROWS, narrow), BF16),
                pltpu.VMEM((layers, mid, narrow), BF16),
                pltpu.VMEM((layers, ROWS, wide), BF16),
                dma((2, 2, 2)),
                dma((2, 2, 4)),
                dma((2,)),
                dma((count, 2)),
                dma((SLOTS, 2, 2)),
                dma((SLOTS, 2, 2, 2)),
                dma((SLOTS, 2)),
                dma((SLOTS, 2, 2)),
                dma((SENT, 2, 2)),
                dma((SENT, 2, 2, 2)),
                dma((SENT, 2)),
                dma((SENT, 2, 2)),
                dma((9, 2)),
                dma((2, 2, 2)),
                dma((2, 2, 2)),
                dma((2, 4)),
                dma((2, 9)),
                dma((count, 2, 9)),
                dma((2,)),
                dma((count, 2)),
                dma,
            ],
            name="fused",
            compiler_params=pltpu.CompilerParams(collective_id=0, has_side_effects=True, vmem_limit_bytes=10 * 2**20),
        )(
            gd.reshape(split_d), gg.reshape(split_g), gu.reshape(split_g), wd.reshape(split_d), wg.reshape(split_g), wu.reshape(split_g),
            md, vd, mg, vg, mu, vu,
        )
        slots = 6
        new_d, new_g, new_u, md, vd, mg, vg, mu, vu = pl.pallas_call(
            functools.partial(put, pieces, slots),
            out_shape=(*(jax.ShapeDtypeStruct(s, BF16) for s in (split_d, split_g, split_g)), *(jax.ShapeDtypeStruct(a.shape, F32) for a in (md, vd, mg, vg, mu, vu))),
            in_specs=[hbm] + [vmem] * 7,
            out_specs=[hbm] * 9,
            scratch_shapes=[pltpu.VMEM((slots, CORES, SIDE, SIDE, *block), BF16), dma((slots,)), dma((slots, CORES)), dma, dma((6,))],
            name="put",
            compiler_params=pltpu.CompilerParams(vmem_limit_bytes=10 * 2**20),
        )(whole, *(pltpu.with_memory_space_constraint(a, pltpu.VMEM) for a in (kept, *moments)))
        md, vd = (a.transpose(1, 0, 2) for a in (md, vd))
        return (new_g.reshape(wg.shape), new_u.reshape(wu.shape), new_d.reshape(wd.shape), mg, mu, md, vg, vu, vd)

    all_of, cut = P(None, None, None), P(None, "dp", None)
    return jax.shard_map(
        step,
        mesh=mesh,
        in_specs=(P(("rep", "dp"), None, None, None),) * 3 + (all_of,) * 3 + (cut,) * 6,
        out_specs=(P("rep", None, None),) * 3 + (P("rep", "dp", None),) * 6,
        check_vma=False,
    )
```

time: 451 us -> 401 us (0.89)
  Pallas kernels: 423 us -> 400 us
  local copies, waits for them, and re-layouts: 22 us -> 0 us
  other arithmetic: 5.16 us -> 0 us
    pallas_call x1, Pallas kernels: 46.3 us -> 31.9 us  [step(): pl.pallas_call(functools.partial(put, pieces, slots), out_shape=(*(jax.Sh...]
    dynamic_update_slice x2 -> x0, local copies, waits for them, and re-layouts: 12.1 us -> none  [shifted(): lax.dynamic_update_slice_in_dim(jnp.zeros((layers, window, narrow), F32),...]
    unnamed x24 -> x0, local copies, waits for them, and re-layouts: 9.64 us -> none
    pallas_call x1, Pallas kernels: 377 us -> 369 us  [step(): pl.pallas_call(functools.partial(fused, pieces), out_shape=(jax.ShapeDtyp...]
    add x2 -> x0, other arithmetic: 5.16 us -> none  [step(): v = [0.95 * a + 0.05 * b * b for a, b in zip((vg, vu, vd), g)]]
where the time goes in v2:
time: 401 us
  Pallas kernels  400 us (100%)
    pallas_call x1, Pallas kernels, step(): pl.pallas_call(functools.partial(fused, pieces), out_shape=(jax.ShapeDtyp...  369 us
    pallas_call x1, Pallas kernels, step(): pl.pallas_call(functools.partial(put, pieces, slots), out_shape=(*(jax.Sh...  31.9 us

profile of v2, /device:TPU:97, one launch (start us, length us, event | category | flops | bytes accessed | tf_op | source)
XLA Modules:
  0.0 401.1 jit_solution(10297492915893192923)
XLA Ops:
  0.6 368.6 %fused.1 = (bf16[21,2,2,4,4,40,640]{6,5,4,3,2,1,0:T(8,128)(2,1)}, bf16[14,2,2,4,4,40,640]{6,5,4,3,2,1,0:T(8,128)(2,1)S(1)}, bf16[21,2,4,4,40,640]{5,4,3,2,1,0:T(...) custom-call(bf16[2,4,4,280,1280]{4,3,2,1,0:T(8,128)(2,1)} %bitcast.1, ...), custom_call_target="tpu_custom_call" | custom-call | tf_op jit(solution)/shard_map/fused/pallas_call | solution.py:551
  369.2 31.9 %put.1 = (bf16[2,4,4,280,1280]{4,3,2,1,0:T(8,128)(2,1)}, bf16[2,4,4,2,40,4480]{5,4,3,2,1,0:T(8,128)(2,1)}, bf16[2,4,4,2,40,4480]{5,4,3,2,1,0:T(8,128)(2,1)}, f32...) custom-call(bf16[21,2,2,4,4,40,640]{6,5,4,3,2,1,0:T(8,128)(2,1)} %ge, ...), custom_call_target="tpu_custom_call" | custom-call | tf_op jit(solution)/shard_map/put/pallas_call | solution.py:602

commit v3 on v2

--- a/solution.py
+++ b/solution.py
@@ -19,14 +19,15 @@
 HELD = LAG[4] + 2
 SENT = 3
 AHEAD = 3
-FROM, TO = 6, 20
+DIRECT, PULLED = 14, 6
+TURNS = 8
 
 
 def fused(pieces, *refs):
     (gd, gg, gu, wd, wg, wu, md, vd, mg, vg, mu, vu, whole, kept, theirs, mbd, vbd, mbg, vbg, mbu, vbu,
-     total, new, got3, gotm, put3, putm, newm, wb3, wbm, wbg,
+     total_ref, new_ref, got3, gotm, put3, putm, newm, wb3, wbm, wbg,
      sem_load, sem_first, sem_swap_s, sem_swap_r, sem_r1, sem_r2, sem_u1, sem_u2, sem_s1, sem_s2, sem_t1, sem_t2,
-     sem_m, sem_xs, sem_xr, sem_own, sem_gs, sem_gr, sem_os, sem_or, sem_kept) = refs
+     sem_m, sem_xs, sem_xr, sem_own, sem_gs, sem_gr, sem_os, sem_or, sem_kept, sem_free) = refs
     count = WEIGHTS * pieces
     me = lax.axis_index("dp")
     x, y, c = me // (CORES * SIDE), (me // CORES) % SIDE, me % CORES
@@ -86,6 +87,12 @@
 
     def t2(q, t, e):
         return kept.at[HELD + 4, t, e, q % SENT, 3]
+
+    def total(q, t):
+        return total_ref.at[q, t]
+
+    def new(q, t):
+        return new_ref.at[q, t]
 
     def of_weight(q, do):
         for w in range(WEIGHTS):
@@ -101,7 +108,7 @@
     def swap(q):
         def do(w, p):
             for t in range(2):
-                send(term(w, t, p, other), theirs.at[q, t], sem_swap_s.at[t], sem_swap_r.at[q, t], partner).start()
+                send(term(w, t, p, other), theirs.at[q, t], sem_swap_s.at[t], sem_swap_r.at[q % TURNS, t], partner).start()
         of_weight(q, do)
 
     def load_own(q):
@@ -113,7 +120,7 @@
     def load(q):
         load_own(q)
         for t in range(2):
-            wait(theirs.at[q, t], sem_swap_r.at[q, t])
+            wait(theirs.at[q, t], sem_swap_r.at[q % TURNS, t])
             pltpu.make_async_copy(theirs.at[q, t], par(q, t), sem_load.at[1, t, q % 2]).start()
 
     def add(dst, *srcs):
@@ -168,6 +175,8 @@
             for k in range(1, 3):
                 chunk(t, k).wait_recv()
             near_chunks(0, t)
+
+    def stage0_rest():
         for t in range(2):
             chunk(t, 3).wait_recv()
             for k in range(4):
@@ -235,7 +244,7 @@
         for t in range(2):
             for e in range(2):
                 wait(u2(q, t, e), sem_u2.at[q % SLOTS, t, e])
-            add(total.at[q, t], u2(q, t, 0), u2(q, t, 1), *cell(q, t, place[t][1]))
+            add(total(q, t), u2(q, t, 0), u2(q, t, 1), *cell(q, t, place[t][1]))
 
     def adamw(dst, w, m, v, g):
         w, g = w.astype(F32), g.astype(F32)
@@ -267,10 +276,10 @@
         copies = []
         for t in range(2):
             if step == 0:
-                three = (total.at[pl.ds((third + 1) * other, third), t], got3.at[t])
-                rest = (total.at[third, t, pl.ds(pl.multiple_of(cut * other, 16), mid)], gotm.at[t])
+                three = (total_ref.at[pl.ds((third + 1) * other, third), t], got3.at[t])
+                rest = (total(third, t).at[pl.ds(pl.multiple_of(cut * other, 16), mid)], gotm.at[t])
             else:
-                three = (put3.at[other, t], new.at[pl.ds((third + 1) * c, third), t])
+                three = (put3.at[other, t], new_ref.at[pl.ds((third + 1) * c, third), t])
                 rest = (putm.at[other, t], newm.at[t])
             copies.append(send(*three, sem_xs.at[step, t, 0], sem_xr.at[step, t, 0], partner))
             copies.append(send(*rest, sem_xs.at[step, t, 1], sem_xr.at[step, t, 1], partner))
@@ -280,7 +289,7 @@
         for t in range(2):
             for k, (piece, r, row, size) in enumerate(parts(c)):
                 for h in range(2):
-                    g = (total.at[piece, t, pl.ds(r, size)], got3.at[t, k] if k < third else gotm.at[t])[h]
+                    g = (total(piece, t).at[pl.ds(r, size)], got3.at[t, k] if k < third else gotm.at[t])[h]
                     half = (c, other)[h]
                     dst = put3.at[half, t, k] if k < third else putm.at[half, t]
                     for b in range(COLS // 128):
@@ -293,13 +302,13 @@
     def merge_d():
         for t in range(2):
             for k in range(third):
-                new[(third + 1) * c + k, t] = put3[c, t, k]
+                new((third + 1) * c + k, t)[...] = put3[c, t, k]
             a, b = putm[c, t], newm[t]
             low, high = jnp.where(c == 0, a, b), jnp.where(c == 0, b, a)
             line = lax.broadcasted_iota(jnp.int32, (mid - cut, COLS), 0)
-            new[third, t, 0:cut] = low[0:cut]
-            new[third, t, cut:mid] = jnp.where(line < top - cut, low[cut:mid].astype(F32), high[0:mid - cut].astype(F32)).astype(BF16)
-            new[third, t, mid:ROWS] = high[mid - cut:mid]
+            new(third, t)[0:cut] = low[0:cut]
+            new(third, t)[cut:mid] = jnp.where(line < top - cut, low[cut:mid].astype(F32), high[0:mid - cut].astype(F32)).astype(BF16)
+            new(third, t)[mid:ROWS] = high[mid - cut:mid]
 
     def loads_g(w):
         (m, v), (mb, vb) = (((mg, vg), (mbg, vbg)), ((mu, vu), (mbu, vbu)))[w - 1]
@@ -315,76 +324,88 @@
                 for b in range(COLS // 128):
                     here, lane = slice(128 * b, 128 * b + 128), slice(COLS * p + 128 * b, COLS * p + 128 * b + 128)
                     mb[t, :, lane], vb[t, :, lane] = adamw(
-                        new.at[w * pieces + p, t, :, here], wbg[t, :, lane], mb[t, :, lane], vb[t, :, lane], total[w * pieces + p, t, :, here])
-
-    def block(q, t, i, j):
+                        new(w * pieces + p, t).at[:, here], wbg[t, :, lane], mb[t, :, lane], vb[t, :, lane], total(w * pieces + p, t)[:, here])
+
+    def piece(q, v):
+        return kept.at[q - DIRECT] if v else whole.at[q]
+
+    def block(q, t, i, j, v):
         a, b = at(t, i, j)
-        return whole.at[q, t, c, a, b]
-
-    def line(q, t, i, h=None):
+        return piece(q, v).at[t, c, a, b]
+
+    def line(q, t, i, v, h=None):
         some = slice(None) if h is None else pl.ds(2 * h, 2)
-        return whole.at[q, t, c, i % SIDE, some] if t == 0 else whole.at[q, t, c, some, i % SIDE]
-
-    def across(q, t, i):
-        send(line(q, t, i), line(q, t, i), sem_os.at[t], sem_or.at[q, t], partner).start()
-
-    def gather0(q):
+        return piece(q, v).at[t, c, i % SIDE, some] if t == 0 else piece(q, v).at[t, c, some, i % SIDE]
+
+    def across(q, t, i, v):
+        send(line(q, t, i, v), line(q, t, i, v), sem_os.at[t], sem_or.at[q % TURNS, t], partner).start()
+
+    def gather0(q, v):
         for t in range(2):
             i, j = place[t]
             for d in range(2):
-                send(new.at[q, t], block(q, t, i, j), sem_gs.at[t, d], sem_gr.at[q, t, d], dev_j(t, (1, 3)[d])).start()
-            pltpu.make_async_copy(new.at[q, t], block(q, t, i, j), sem_own.at[t, q % 4]).start()
-
-    def gather1(q):
+                send(new(q, t), block(q, t, i, j, v), sem_gs.at[t, d], sem_gr.at[q % TURNS, t, d], dev_j(t, (1, 3)[d])).start()
+            if v:
+                block(q, t, i, j, v)[...] = new(q, t)[...]
+            else:
+                pltpu.make_async_copy(new(q, t), block(q, t, i, j, v), sem_own.at[t, q % 4]).start()
+
+    def gather1(q, v):
         for t in range(2):
             i, j = place[t]
-            wait(new.at[q, t], sem_gr.at[q, t, 0])
-            wait(new.at[q, t], sem_gr.at[q, t, 1])
-            src = block(q, t, i, j + SIDE - side(q))
-            send(src, src, sem_gs.at[t, 2], sem_gr.at[q, t, 2], dev_j(t, side(q))).start()
-            wait(new.at[q, t], sem_own.at[t, q % 4])
-
-    def gather2(q):
-        for t in range(2):
-            i = place[t][0]
-            wait(new.at[q, t], sem_gr.at[q, t, 2])
+            wait(new(q, t), sem_gr.at[q % TURNS, t, 0])
+            wait(new(q, t), sem_gr.at[q % TURNS, t, 1])
+            src = block(q, t, i, j + side(q), v)
+            send(src, src, sem_gs.at[t, 2], sem_gr.at[q % TURNS, t, 2], dev_j(t, SIDE - side(q))).start()
+            if not v:
+                wait(new(q, t), sem_own.at[t, q % 4])
+
+    def gather2(q, v):
+        for t in range(2):
+            wait(new(q, t), sem_gr.at[q % TURNS, t, 2])
             for k in range(2):
                 for d in range(2):
-                    half = line(q, t, i, (d, 1 - d)[k])
-                    send(half, half, sem_gs.at[t, 3 + 2 * k + d], sem_gr.at[q, t, 3 + 2 * k + d], dev_i(t, (1, 3)[d])).start()
-            across(q, t, i)
-
-    def gather3(q):
-        for t in range(2):
-            for d in range(2):
-                half = line(q, t, place[t][0] + (3, 1)[d], d)
-                wait(half, sem_gr.at[q, t, 3 + d])
-                send(half, half, sem_gs.at[t, 7 + d], sem_gr.at[q, t, 7 + d], dev_i(t, (1, 3)[d])).start()
+                    half = line(q, t, place[t][0], v, (d, 1 - d)[k])
+                    send(half, half, sem_gs.at[t, 3 + 2 * k + d], sem_gr.at[q % TURNS, t, 3 + 2 * k + d], dev_i(t, (1, 3)[d])).start()
+            across(q, t, place[t][0], v)
+
+    def gather3(q, v):
+        for t in range(2):
+            for d in range(2):
+                half = line(q, t, place[t][0] + (3, 1)[d], v, d)
+                wait(half, sem_gr.at[q % TURNS, t, 3 + d])
+                send(half, half, sem_gs.at[t, 7 + d], sem_gr.at[q % TURNS, t, 7 + d], dev_i(t, (1, 3)[d])).start()
         for t in range(2):
             for d in range(2):
                 there = place[t][0] + (3, 1)[d]
-                wait(line(q, t, there, 1 - d), sem_gr.at[q, t, 5 + d])
-                across(q, t, there)
-
-    def gather4(q):
-        for t in range(2):
-            i = place[t][0]
-            for d in range(2):
-                wait(line(q, t, i + 2, d), sem_gr.at[q, t, 7 + d])
-            across(q, t, i + 2)
-
-    def keep(q):
-        for t in range(2):
-            wait(whole.at[q, t, other], sem_or.at[q, t])
-
-        @pl.when(jnp.logical_and(q >= FROM, q < TO))
-        def _():
-            pltpu.make_async_copy(whole.at[q], kept.at[q - FROM], sem_kept).start()
+                wait(line(q, t, there, v, 1 - d), sem_gr.at[q % TURNS, t, 5 + d])
+                across(q, t, there, v)
+
+    def gather4(q, v):
+        for t in range(2):
+            there = place[t][0] + 2
+            for d in range(2):
+                wait(line(q, t, there, v, d), sem_gr.at[q % TURNS, t, 7 + d])
+            across(q, t, there, v)
+
+    def keep(q, v):
+        for t in range(2):
+            wait(piece(q, v).at[t, other], sem_or.at[q % TURNS, t])
+        if not v:
+            @pl.when(q >= PULLED)
+            def _():
+                pltpu.make_async_copy(whole.at[q], kept.at[q - PULLED + count - DIRECT], sem_kept).start()
 
     def when(q, do):
         @pl.when(jnp.logical_and(q >= 0, q < count))
         def _():
             do(q)
+
+    def each(q, do):
+        for v in range(2):
+            @pl.when(jnp.logical_and(q >= DIRECT * v, q < (DIRECT, count)[v]))
+            def _(v=v):
+                do(q, v == 1)
 
     def on(tick, t, do):
         @pl.when(t == tick)
@@ -397,20 +418,26 @@
     for peer in peers:
         pl.semaphore_signal(barrier, inc=1, device_id={"dp": peer}, device_id_type=MESH)
     pl.semaphore_wait(barrier, len(peers))
-    for k in range(4):
+    for k in range(3):
         for t in range(2):
             chunk(t, k).start()
-    for q in range(1, AHEAD):
+    swap(1)
+    for t in range(2):
+        chunk(t, 3).start()
+    for q in range(2, AHEAD):
         swap(q)
     for copy in loads_d() + loads_g(1) + loads_g(2) + [load_w(1)]:
         copy.start()
     stage0_first()
+    stage1(0)
+    stage0_rest()
 
     ends = [w * pieces + pieces - 1 + LAG[4] for w in range(WEIGHTS)]
     gathers = ends[0] + 2
+    clear = ends[-1] + 1
     stages = (stage0, stage1, stage2, stage3, stage4)
     rounds = (gather0, gather1, gather2, gather3, gather4, keep)
-    assert FROM + gathers + ROUND[5] > ends[-1] + 1 and TO - FROM == kept.shape[0] and HELD + 6 <= TO - FROM
+    assert PULLED + gathers + ROUND[5] > clear and kept.shape[0] == count - PULLED and count - DIRECT == HELD + 1
 
     def start(copies):
         for copy in copies:
@@ -450,13 +477,22 @@
                         wait(s2(z, t, d, h), sem_s2.at[z, t, d, h])
                 wait(t1(z, t), sem_t1.at[z, t])
 
+    def cleared():
+        sent()
+        pl.semaphore_signal(sem_free, inc=1, device_id={"dp": partner}, device_id_type=MESH)
+
     def tick(t, _):
         when(t + AHEAD, swap)
         when(t + 1, load)
+        on(DIRECT + gathers + ROUND[2], t, lambda: pl.semaphore_wait(sem_free, 1))
         for k in range(5, 0, -1):
-            when(t - gathers - ROUND[k], rounds[k])
-        for k in range(4, 0, -1):
+            each(t - gathers - ROUND[k], rounds[k])
+        for k in range(4, 1, -1):
             when(t - LAG[k], stages[k])
+
+        @pl.when(t > LAG[1])
+        def _():
+            when(t - LAG[1], stage1)
 
         @pl.when(t > 0)
         def _():
@@ -466,8 +502,8 @@
         on(ends[0] + 2, t, d_end)
         for w in range(1, WEIGHTS):
             on(ends[w], t, functools.partial(g_step, w))
-        on(ends[-1] + 1, t, sent)
-        when(t - gathers, gather0)
+        on(clear, t, cleared)
+        each(t - gathers, gather0)
         return 0
 
     lax.fori_loop(0, count + gathers + ROUND[5], tick, 0)
@@ -475,17 +511,16 @@
     for t in range(2):
         wait(theirs.at[1:, t], sem_swap_s.at[t])
         for k in range(3):
-            wait(new.at[:, t], sem_gs.at[t, k])
-        for d in range(2):
-            for k in range(3):
-                wait(whole.at[:, t, c, 0, 0:2], sem_gs.at[t, 3 + 2 * k + d])
-        wait(whole.at[:, t, c], sem_os.at[t])
-    wait(kept, sem_kept)
+            wait(theirs.at[:, t, 0, 0], sem_gs.at[t, k])
+        for k in range(3, 9):
+            wait(theirs.at[:, t, 0, 0:2], sem_gs.at[t, k])
+        wait(theirs.at[:, t], sem_os.at[t])
+    wait(kept.at[0:DIRECT - PULLED], sem_kept)
 
 
 def put(pieces, slots, whole, kept, mbd, vbd, mbg, vbg, mbu, vbu, out_d, out_g, out_u, md, vd, mg, vg, mu, vu, buf, sem_in, sem_out, sem_kept, sem_m):
-    steps = [(q, t) for q in range(WEIGHTS * pieces) for t in range(2) if not FROM <= q < TO]
-    rest = [(q, t) for q in range(FROM, TO) for t in range(2)]
+    steps = [(q, t, c) for q in range(PULLED) for t in range(2) for c in range(CORES)]
+    rest = [(q, t, c) for q in range(PULLED, WEIGHTS * pieces) for t in range(2) for c in range(CORES)]
 
     def dst(q, t, c):
         w, p = divmod(q, pieces)
@@ -494,11 +529,10 @@
         return (out_g, out_u)[w - 1].at[t, :, :, c, :, COLS * p:COLS * p + COLS]
 
     def load(s):
-        q, t = steps[s]
-        return pltpu.make_async_copy(whole.at[q, t], buf.at[s % slots], sem_in.at[s % slots])
-
-    def stores(s):
-        return [pltpu.make_async_copy(buf.at[s % slots, c], dst(*steps[s], c), sem_out.at[s % slots, c]) for c in range(CORES)]
+        return pltpu.make_async_copy(whole.at[steps[s]], buf.at[s % slots], sem_in.at[s % slots])
+
+    def store(s):
+        return pltpu.make_async_copy(buf.at[s % slots], dst(*steps[s]), sem_out.at[s % slots])
 
     mine = pl.ds((mbd.shape[0] - md.shape[0]) * (lax.axis_index("dp") % CORES), md.shape[0])
     moments = [(mbd.at[mine], md), (vbd.at[mine], vd), (mbg, mg), (vbg, vg), (mbu, mu), (vbu, vu)]
@@ -509,20 +543,17 @@
     for copy in moments:
         copy.start()
     for s in range(len(steps)):
-        for q, t in rest[len(rest) * s // len(steps):len(rest) * (s + 1) // len(steps)]:
-            for c in range(CORES):
-                pltpu.make_async_copy(kept.at[q - FROM, t, c], dst(q, t, c), sem_kept).start()
+        for q, t, c in rest[len(rest) * s // len(steps):len(rest) * (s + 1) // len(steps)]:
+            slot = q - DIRECT if q >= DIRECT else q - PULLED + WEIGHTS * pieces - DIRECT
+            pltpu.make_async_copy(kept.at[slot, t, c], dst(q, t, c), sem_kept).start()
         if s + ahead < len(steps):
             if s + ahead >= slots:
-                for copy in stores(s + ahead - slots):
-                    copy.wait()
+                store(s + ahead - slots).wait()
             load(s + ahead).start()
         load(s).wait()
-        for copy in stores(s):
-            copy.start()
+        store(s).start()
     for s in range(max(0, len(steps) - slots), len(steps)):
-        for copy in stores(s):
-            copy.wait()
+        store(s).wait()
     pltpu.make_async_copy(kept, kept, sem_kept).wait()
     for copy in moments:
         copy.wait()
@@ -551,8 +582,8 @@
         whole, kept, _, *moments = pl.pallas_call(
             functools.partial(fused, pieces),
             out_shape=(
-                jax.ShapeDtypeStruct((count, 2, CORES, SIDE, SIDE, *block), BF16),
-                pltpu.VMEM((TO - FROM, 2, CORES, SIDE, SIDE, *block), BF16),
+                jax.ShapeDtypeStruct((DIRECT, 2, CORES, SIDE, SIDE, *block), BF16),
+                pltpu.VMEM((count - PULLED, 2, CORES, SIDE, SIDE, *block), BF16),
                 jax.ShapeDtypeStruct((count, 2, SIDE, SIDE, *block), BF16),
                 *(pltpu.VMEM((window, *md.shape[1:]), F32) for _ in range(2)),
                 *(pltpu.VMEM(mg.shape, F32) for _ in range(4)),
@@ -573,7 +604,7 @@
                 dma((2, 2, 2)),
                 dma((2, 2, 4)),
                 dma((2,)),
-                dma((count, 2)),
+                dma((TURNS, 2)),
                 dma((SLOTS, 2, 2)),
                 dma((SLOTS, 2, 2, 2)),
                 dma((SLOTS, 2)),
@@ -587,26 +618,27 @@
                 dma((2, 2, 2)),
                 dma((2, 4)),
                 dma((2, 9)),
-                dma((count, 2, 9)),
+                dma((TURNS, 2, 9)),
                 dma((2,)),
-                dma((count, 2)),
+                dma((TURNS, 2)),
                 dma,
+                pltpu.SemaphoreType.REGULAR,
             ],
             name="fused",
-            compiler_params=pltpu.CompilerParams(collective_id=0, has_side_effects=True, vmem_limit_bytes=10 * 2**20),
+            compiler_params=pltpu.CompilerParams(collective_id=0, has_side_effects=True, vmem_limit_bytes=8 * 2**20),
         )(
             gd.reshape(split_d), gg.reshape(split_g), gu.reshape(split_g), wd.reshape(split_d), wg.reshape(split_g), wu.reshape(split_g),
             md, vd, mg, vg, mu, vu,
         )
-        slots = 6
+        slots = 9
         new_d, new_g, new_u, md, vd, mg, vg, mu, vu = pl.pallas_call(
             functools.partial(put, pieces, slots),
             out_shape=(*(jax.ShapeDtypeStruct(s, BF16) for s in (split_d, split_g, split_g)), *(jax.ShapeDtypeStruct(a.shape, F32) for a in (md, vd, mg, vg, mu, vu))),
             in_specs=[hbm] + [vmem] * 7,
             out_specs=[hbm] * 9,
-            scratch_shapes=[pltpu.VMEM((slots, CORES, SIDE, SIDE, *block), BF16), dma((slots,)), dma((slots, CORES)), dma, dma((6,))],
+            scratch_shapes=[pltpu.VMEM((slots, SIDE, SIDE, *block), BF16), dma((slots,)), dma((slots,)), dma, dma((6,))],
             name="put",
-            compiler_params=pltpu.CompilerParams(vmem_limit_bytes=10 * 2**20),
+            compiler_params=pltpu.CompilerParams(vmem_limit_bytes=8 * 2**20),
         )(whole, *(pltpu.with_memory_space_constraint(a, pltpu.VMEM) for a in (kept, *moments)))
         md, vd = (a.transpose(1, 0, 2) for a in (md, vd))
         return (new_g.reshape(wg.shape), new_u.reshape(wu.shape), new_d.reshape(wd.shape), mg, mu, md, vg, vu, vd)

time: 401 us -> 395 us (0.985)
  Pallas kernels: 400 us -> 394 us
    pallas_call x1, Pallas kernels: 369 us -> 363 us  [step(): pl.pallas_call(functools.partial(fused, pieces), out_shape=(jax.ShapeDtyp...]
where the time goes in v3:
time: 395 us
  Pallas kernels  394 us (100%)
    pallas_call x1, Pallas kernels, step(): pl.pallas_call(functools.partial(fused, pieces), out_shape=(jax.ShapeDtyp...  363 us
    pallas_call x1, Pallas kernels, step(): pl.pallas_call(functools.partial(put, pieces, slots), out_shape=(*(jax.Sh...  30.9 us

profile of v3, /device:TPU:97, one launch (start us, length us, event | category | flops | bytes accessed | tf_op | source)
XLA Modules:
  0.0 394.8 jit_solution(14671571701132257977)
XLA Ops:
  0.6 363.3 %fused.1 = (bf16[14,2,2,4,4,40,640]{6,5,4,3,2,1,0:T(8,128)(2,1)}, bf16[15,2,2,4,4,40,640]{6,5,4,3,2,1,0:T(8,128)(2,1)S(1)}, bf16[21,2,4,4,40,640]{5,4,3,2,1,0:T(...) custom-call(bf16[2,4,4,280,1280]{4,3,2,1,0:T(8,128)(2,1)} %bitcast.1, ...), custom_call_target="tpu_custom_call" | custom-call | tf_op jit(solution)/shard_map/fused/pallas_call | solution.py:582
  363.9 30.9 %put.1 = (bf16[2,4,4,280,1280]{4,3,2,1,0:T(8,128)(2,1)}, bf16[2,4,4,2,40,4480]{5,4,3,2,1,0:T(8,128)(2,1)}, bf16[2,4,4,2,40,4480]{5,4,3,2,1,0:T(8,128)(2,1)}, f32...) custom-call(bf16[14,2,2,4,4,40,640]{6,5,4,3,2,1,0:T(8,128)(2,1)} %ge, ...), custom_call_target="tpu_custom_call" | custom-call | tf_op jit(solution)/shard_map/put/pallas_call | solution.py:634
